TPU v7x, 32 devices: a whole 2x2x4 slice. The times are simulated.
32 devices in a mesh: section: 8 (over y, x, core), tensor: 4 (over z).
Axes of the slice: x: 2, y: 2, z: 4, core: 2. Of those that a mesh axis runs over, the one named last changes fastest.
Arguments:
- section_inputs: bfloat16 [8, 512, 1024], P('section', 'tensor'), may hold values from -6 to 6
- w_in: bfloat16 [8, 2304, 1024], P('section', 'tensor'), may hold values from -0.1875 to 0.1875
- in_bias: bfloat16 [8, 2304], P('section', 'tensor'), may hold values from -3 to 3
- w_out: bfloat16 [8, 2304, 1024], P('section', 'tensor'), may hold values from -0.125 to 0.125
- out_bias: float32 [8, 1024], P('section'), may hold values from -2 to 2
- norm_gain: float32 [8, 1024], P('section'), may hold values from 0.1 to 1.9
- norm_bias: float32 [8, 1024], P('section'), may hold values from -2 to 2
- patches: bfloat16 [8, 512, 1024], P(None, 'tensor'), may hold values from -6 to 6
- plan: int32 [3], replicated, may hold values from 0 to 7, as said below
Outputs:
- received: bfloat16 [8, 4, 512, 1024], P('section', None, 'tensor')
Inputs may be any that keep to these rules, and one draw needn't show every extreme that they name: `plan`: the first min(8, 3) entries are all different.
All inputs are finite; a program needn't handle non-finite values.
Results may differ from a plain program's by a relative error of at most 0.0065.
Values may be sent and summed in bfloat16 or wider, within the bound.
A program may use at most 64 MiB of HBM per device.

v0:
```python
import functools

import jax
import jax.numpy as jnp
from jax import lax
from jax.experimental import pallas as pl
from jax.experimental.pallas import tpu as pltpu
from jax.sharding import PartitionSpec as P

TICKS = 4
PIECES = 4
HOP_SLOTS = 2
VMEM_BYTES = 60 * 1024 * 1024

norm_floor = 0.1
gelu_slope = 1.702
MESH = pl.DeviceIdType.MESH


def activate(preact):
    return preact * jax.nn.sigmoid(gelu_slope * preact)


def normalize(widened, gain_row, shift_row):
    average = jnp.mean(widened, axis=-1, keepdims=True)
    centered = widened - average
    variance = jnp.mean(centered * centered, axis=-1, keepdims=True)
    return (centered * lax.rsqrt(variance + norm_floor) * gain_row + shift_row).astype(
        jnp.bfloat16
    )


def relay_kernel(
    n, sections, hop_slots,
    x_ref, win_hbm, ib_ref, wout_hbm, ob_ref, gain_ref, shift_ref, patches_hbm, plan_ref,
    o_ref,
    win_ref, wout_ref, patches_ref, load_sem, held, sums_in, sums_out, staged, total,
    x_send, x_recv, sum_send, sum_recv, ship_send, final_recv,
):
    pieces = x_ref.shape[0]
    chunks = n // 2 * pieces
    items = TICKS * chunks
    me = lax.axis_index("tensor")
    section = lax.axis_index("section")
    following = lax.rem(section + 1, sections)
    preceding = lax.rem(section + sections - 1, sections)

    loads = [
        pltpu.make_async_copy(source, target, load_sem.at[index])
        for index, (source, target) in enumerate(
            [(win_hbm, win_ref), (wout_hbm, wout_ref), (patches_hbm, patches_ref)]
        )
    ]
    for load in loads[:2]:
        load.start()
    pl.when(section == 0)(loads[2].start)

    barrier = pltpu.get_barrier_semaphore()

    def greet(sect, tensor):
        pl.semaphore_signal(
            barrier, inc=1, device_id={"section": sect, "tensor": tensor}, device_id_type=MESH
        )

    for tensor in range(n):
        greet(following, tensor)
        greet(preceding, tensor)
        pl.when(me != tensor)(functools.partial(greet, section, tensor))
    pl.semaphore_wait(barrier, 3 * n - 1)

    def x_copy(src, group, item, sect, tensor, send_sem):
        return pltpu.make_async_remote_copy(
            src_ref=src,
            dst_ref=held.at[group, item],
            send_sem=send_sem,
            recv_sem=x_recv.at[group, item],
            device_id={"section": sect, "tensor": tensor},
            device_id_type=MESH,
        )

    def forward_copy(group, item, tensor):
        return x_copy(
            held.at[group, item], group, item, section, tensor, x_send.at[group, item]
        )

    def relay_copy(group, item):
        return x_copy(
            sums_out.at[group, item], group, item + chunks, following, me,
            sum_send.at[group, item],
        )

    def sum_copy(group, item, tensor):
        return pltpu.make_async_remote_copy(
            src_ref=sums_out.at[group, item],
            dst_ref=sums_in.at[group, item],
            send_sem=sum_send.at[group, item],
            recv_sem=sum_recv.at[group, item],
            device_id={"section": section, "tensor": tensor},
            device_id_type=MESH,
        )

    def final_copy(group, item, tick, piece, home):
        return pltpu.make_async_remote_copy(
            src_ref=sums_out.at[group, item],
            dst_ref=o_ref.at[tick, piece],
            send_sem=sum_send.at[group, item],
            recv_sem=final_recv.at[tick, piece],
            device_id={"section": following, "tensor": home},
            device_id_type=MESH,
        )

    def entry_side(origin):
        later = sections - 1 - origin
        far = (origin >= 0) & (later < TICKS) & (lax.rem(later, 2) == 0)
        return far.astype(jnp.int32)

    def place(group, item):
        tick, chunk = lax.div(item, chunks), lax.rem(item, chunks)
        shard, piece = lax.div(chunk, pieces), lax.rem(chunk, pieces)
        home = jnp.where(group == 0, shard, n - 1 - shard)
        turns = jnp.minimum(tick, section) + entry_side(section - tick) + group
        right = lax.rem(turns, 2) == 0
        position = jnp.where(right, me, n - 1 - me)
        target = jnp.where(right, me + 1, me - 1)
        return tick, piece, home, position, target

    my_group = jnp.where(me < n // 2, 0, 1)
    my_start = lax.rem(my_group + entry_side(section), 2) * (n - 1)
    my_side = my_group * (n - 1)
    my_first = jnp.where(me < n // 2, me, n - 1 - me) * pieces

    def enter(tick, piece, carry):
        item = tick * chunks + my_first + piece
        if tick == 0:
            source, start = x_ref.at[piece], my_start
        else:
            start = my_side
            source = staged.at[tick - 1, piece]
            staged[tick - 1, piece] = patches_ref[plan_ref[tick - 1], piece]

        held[my_group, item] = source[...]

        @pl.when(me != start)
        def _():
            x_copy(
                source, my_group, item, section, start, ship_send.at[tick, piece]
            ).start()

        return carry

    lax.fori_loop(0, pieces, functools.partial(enter, 0), 0)

    @pl.when(section == 0)
    def _():
        loads[2].wait()
        for tick in range(1, TICKS):
            lax.fori_loop(0, pieces, functools.partial(enter, tick), 0)

    def receive(group, item, position):
        tick, piece, home, where, target = place(group, item)

        @pl.when(where == position)
        def _():
            entry = (tick == 0) | (section == 0)

            @pl.when(jnp.logical_not(entry & (home == me)))
            def _():
                forward_copy(group, item, target).wait_recv()

            @pl.when((position < n - 1) & jnp.logical_not(entry & (home == target)))
            def _():
                forward_copy(group, item, target).start()

            @pl.when((tick > 0) & (section > 0) & (home == me))
            def _():
                o_ref[tick - 1, piece] = held[group, item]

    def compute(group, item, position):
        tick, piece, home, where, target = place(group, item)

        @pl.when(where == position)
        def _():
            normed = normalize(
                held[group, item].astype(jnp.float32), gain_ref[...], shift_ref[...]
            )
            preact = lax.dot_general(
                normed, win_ref[...], (((1,), (1,)), ((), ())),
                preferred_element_type=jnp.float32,
            )
            hidden = activate(preact + ib_ref[...].astype(jnp.float32)).astype(jnp.bfloat16)
            total[...] = jnp.dot(hidden, wout_ref[...], preferred_element_type=jnp.float32)

            @pl.when(position > 0)
            def _():
                sum_copy(group, item, target).wait_recv()
                total[...] += sums_in[group, item].astype(jnp.float32)

            @pl.when(position < n - 1)
            def _():
                sums_out[group, item] = total[...].astype(jnp.bfloat16)
                sum_copy(group, item, target).start()

            @pl.when(position == n - 1)
            def _():
                sums_out[group, item] = (
                    held[group, item].astype(jnp.float32) + total[...] + ob_ref[...]
                ).astype(jnp.bfloat16)
                leaves = (tick == TICKS - 1) | (following == 0)

                @pl.when(leaves)
                def _():
                    final_copy(group, item, tick, piece, home).start()

                @pl.when(jnp.logical_not(leaves))
                def _():
                    relay_copy(group, item).start()

    def each(action, slot):
        def one(index, carry):
            group, position = lax.rem(index, 2), lax.div(index, 2)
            item = slot - position * hop_slots
            pl.when((item >= 0) & (item < items))(
                functools.partial(action, group, item, position)
            )
            return carry

        lax.fori_loop(0, 2 * n, one, 0)

    def turn(slot, carry):
        each(compute, slot)
        each(receive, slot + 1)
        return carry

    each(receive, 0)
    for load in loads[:2]:
        load.wait()
    lax.fori_loop(0, items + (n - 1) * hop_slots, turn, 0)

    def drain(item, carry):
        for group in range(2):
            tick, piece, home, position, target = place(group, item)

            entry = (tick == 0) | (section == 0)

            @pl.when((position < n - 1) & jnp.logical_not(entry & (home == target)))
            def _():
                forward_copy(group, item, target).wait_send()

            sum_copy(group, item, target).wait_send()

            @pl.when((home == me) & ((tick == TICKS - 1) | (section == 0)))
            def _():
                final_copy(group, item, tick, piece, home).wait_recv()

            start = jnp.where(tick == 0, my_start, my_side)
            sent = (home == me) & (me != start) & entry

            @pl.when(sent)
            def _():
                x_copy(
                    staged.at[0, piece], group, item, section, start,
                    ship_send.at[tick, piece],
                ).wait_send()

        return carry

    lax.fori_loop(0, items, drain, 0)


def relay_call(n, sections, pieces, hop_slots, args):
    x, w_in, in_bias, w_out, out_bias, gain, shift, patches, plan = args
    tokens, width = x.shape
    rows = tokens // pieces
    items = TICKS * n // 2 * pieces
    micro = patches.shape[0]
    bf16 = jnp.bfloat16
    vmem = pl.BlockSpec(memory_space=pltpu.VMEM)
    hbm = pl.BlockSpec(memory_space=pl.ANY)
    every = (2, items, rows, width)
    dma = pltpu.SemaphoreType.DMA
    out = pl.pallas_call(
        functools.partial(relay_kernel, n, sections, hop_slots),
        out_shape=jax.ShapeDtypeStruct((TICKS, pieces, rows, width), bf16),
        in_specs=[vmem, hbm, vmem, hbm, vmem, vmem, vmem, hbm]
        + [pl.BlockSpec(memory_space=pltpu.SMEM)],
        out_specs=vmem,
        scratch_shapes=[
            pltpu.VMEM(w_in.shape, bf16),
            pltpu.VMEM(w_out.shape, bf16),
            pltpu.VMEM((micro, pieces, rows, width), bf16),
            dma((3,)),
            pltpu.VMEM(every, bf16),
            pltpu.VMEM(every, bf16),
            pltpu.VMEM(every, bf16),
            pltpu.VMEM((TICKS - 1, pieces, rows, width), bf16),
            pltpu.VMEM((rows, width), jnp.float32),
            dma((2, items)),
            dma((2, items)),
            dma((2, items)),
            dma((2, items)),
            dma((TICKS, pieces)),
            dma((TICKS, pieces)),
        ],
        compiler_params=pltpu.CompilerParams(
            collective_id=0, has_side_effects=True, vmem_limit_bytes=VMEM_BYTES
        ),
    )(
        x.reshape(pieces, rows, width),
        w_in,
        in_bias.reshape(1, -1),
        w_out,
        out_bias.reshape(1, -1),
        gain.reshape(1, -1),
        shift.reshape(1, -1),
        patches.reshape(micro, pieces, rows, width),
        plan,
    )
    return out.reshape(1, TICKS, tokens, width)


def passed_along(value, axis, steps):
    count = lax.axis_size(axis)
    pairs = [(source, (source + steps) % count) for source in range(count)]
    return lax.ppermute(value, axis, pairs)


def gathered_weights(args):
    current, w_in, in_bias, w_out, bias_row, gain_row, shift_row, patches, plan = args
    section_index = lax.axis_index("section")
    full_in, full_bias, full_out = (
        lax.all_gather(value, "tensor", axis=0, tiled=True) for value in (w_in, in_bias, w_out)
    )
    records = []
    for tick_index in range(TICKS):
        widened = current.astype(jnp.float32)
        normed = normalize(widened, gain_row, shift_row)
        preact = lax.dot_general(
            normed, full_in, (((1,), (1,)), ((), ())), preferred_element_type=jnp.float32
        )
        hidden = activate(preact + full_bias.astype(jnp.float32)).astype(jnp.bfloat16)
        produced = (
            widened + jnp.dot(hidden, full_out, preferred_element_type=jnp.float32) + bias_row
        ).astype(jnp.bfloat16)
        arrived = passed_along(produced, "section", 1)
        records.append(arrived)
        if tick_index + 1 < TICKS:
            selected = lax.dynamic_index_in_dim(patches, plan[tick_index], 0, keepdims=False)
            current = jnp.where(section_index == 0, selected, arrived)
    return jnp.stack(records, axis=0)[None]


def shards(n, sections, *blocks):
    args = tuple(block[0] for block in blocks[:7]) + blocks[7:]
    tokens, width = args[0].shape
    room = 2 * width * (
        tokens * (TICKS * (3 * n + 2) + 1 + args[7].shape[0]) + 2 * args[1].shape[0]
    )
    if tokens % (PIECES * 16) or n % 2 or sections < 2 or room > VMEM_BYTES * 3 // 4:
        return gathered_weights(args)
    return relay_call(n, sections, PIECES, HOP_SLOTS, args)


def solution(mesh):
    placed = (
        P("section", "tensor", None),
        P("section", "tensor", None),
        P("section", "tensor"),
        P("section", "tensor", None),
        P("section", None),
        P("section", None),
        P("section", None),
        P(None, "tensor", None),
        P(),
    )
    return jax.shard_map(
        functools.partial(shards, mesh.shape["tensor"], mesh.shape["section"]),
        mesh=mesh,
        in_specs=placed,
        out_specs=P("section", None, "tensor", None),
        check_vma=False,
    )
```

profile of v0, /device:TPU:17, one launch (start us, length us, event | category | flops | bytes accessed | tf_op | source)
XLA Modules:
  0.0 122.5 jit_solution(7348716928373447908)
XLA Ops:
  0.0 120.2 %shard_map.91 = bf16[4,4,32,1024]{3,2,1,0:T(8,128)(2,1)} custom-call(bf16[4,32,1024]{2,1,0:T(8,128)(2,1)} %bitcast.9, bf16[576,1024]{1,0:T(8,128)(2,1)} %bitcast.7, bf16[1,576]{1,0:T(2,128)(2,1)} %ib_ref.1, bf16[576,1024]{1,0:T(8,128)(2,1)} %bitcast.8, f32[1,1024]{1,0:T(1,128)} %ob_ref.1, f32[1,1024]{1,0:T(1,128)} %gain_ref.1, f32[1,1024]{1,0:T(1,128)} %shift_ref.1, ...), custom_call_target="tpu_custom_call" | custom-call | tf_op jit(solution)/shard_map/pallas_call | solution.py:281
  120.2 2.3 %copy.11 = bf16[1,4,128,1024]{3,2,1,0:T(8,128)(2,1)} copy(bf16[1,4,128,1024]{3,2,1,0:T(8,128)(2,1)} %bitcast.5) | data formatting | bytes 2097152
where the time goes:
time: 123 us; the launch traced here: 122 us
  Pallas kernels  120 us (98%)
  local copies, waits for them, and re-layouts  2.26 us (2%)
    pallas_call x1, Pallas kernels, relay_call(): pl.pallas_call(functools.partial(relay_kernel, n, sections, hop_slots), o...  120 us

commit v1 on v0

v1 whole, which is shorter than its diff:
```python
import functools

import jax
import jax.numpy as jnp
from jax import lax
from jax.experimental import pallas as pl
from jax.experimental.pallas import tpu as pltpu
from jax.sharding import PartitionSpec as P

TICKS = 4
PIECES = 4
HOP_SLOTS = 2
SETTLE_LAG = 3
PASS_LAG = 2
VMEM_BYTES = 60 * 1024 * 1024

norm_floor = 0.1
gelu_slope = 1.702
MESH = pl.DeviceIdType.MESH


def activate(preact):
    return preact * jax.nn.sigmoid(gelu_slope * preact)


def normalize(widened, gain_row, shift_row):
    average = jnp.mean(widened, axis=-1, keepdims=True)
    centered = widened - average
    variance = jnp.mean(centered * centered, axis=-1, keepdims=True)
    return (centered * lax.rsqrt(variance + norm_floor) * gain_row + shift_row).astype(
        jnp.bfloat16
    )


def relay_kernel(
    n, sections, hop_slots,
    x_ref, win_hbm, ib_ref, wout_hbm, ob_ref, gain_ref, shift_ref, patches_hbm, plan_ref,
    o_ref,
    win_ref, wout_ref, patches_ref, load_sem, held, sums_in, sums_out, staged, passing, total,
    x_send, x_recv, sum_send, sum_recv, ship_send, pass_send, pass_recv, final_recv,
):
    pieces, rows = x_ref.shape[0], x_ref.shape[1]
    near, far = n // 2 - 1, n // 2
    chunks = n // 2 * pieces
    items = TICKS * chunks
    me = lax.axis_index("tensor")
    section = lax.axis_index("section")
    following = lax.rem(section + 1, sections)
    preceding = lax.rem(section + sections - 1, sections)
    carriers = [2 * tick % sections for tick in range(1, TICKS)]

    carries = section == 0
    for carrier in carriers:
        carries = carries | (section == carrier)

    loads = [
        pltpu.make_async_copy(source, target, load_sem.at[index])
        for index, (source, target) in enumerate(
            [(win_hbm, win_ref), (wout_hbm, wout_ref), (patches_hbm, patches_ref)]
        )
    ]
    for load in loads[:2]:
        load.start()
    pl.when(carries)(loads[2].start)

    def entry_side(origin):
        length = jnp.minimum(TICKS, sections - origin)
        return jnp.where(origin >= 0, lax.rem(length, 2), 0)

    def start_of(group, origin):
        return jnp.where(lax.rem(group + entry_side(origin), 2) == 0, near, far)

    my_group = jnp.where(me < n // 2, 0, 1)
    my_shard = jnp.where(me < n // 2, me, n - 1 - me)
    my_start = start_of(my_group, section)
    my_side = jnp.where(me < n // 2, near, far)

    barrier = pltpu.get_barrier_semaphore()

    def greet(sect, tensor):
        pl.semaphore_signal(
            barrier, inc=1, device_id={"section": sect, "tensor": tensor}, device_id_type=MESH
        )

    greet(following, me)
    greet(preceding, me)
    pl.when(me > 0)(lambda: greet(section, me - 1))
    pl.when(me < n - 1)(lambda: greet(section, me + 1))
    for home in range(n):
        group = home * 2 // n
        distant = jnp.abs(me - home) > 1
        pl.when(distant & (me == start_of(group, section)))(
            functools.partial(greet, section, home)
        )
        for carrier in carriers:
            if carrier and home != (near, far)[group]:
                pl.when((section == 0) & (me == (near, far)[group]))(
                    functools.partial(greet, carrier, home)
                )
    expected = 4 - jnp.where((me == 0) | (me == n - 1), 1, 0)
    expected = expected + jnp.where(jnp.abs(me - my_start) > 1, 1, 0)
    for carrier in carriers:
        if carrier:
            expected = expected + jnp.where((section == carrier) & (me != my_side), 1, 0)
    pl.semaphore_wait(barrier, expected)

    def x_copy(src, group, item, sect, tensor, send_sem):
        return pltpu.make_async_remote_copy(
            src_ref=src,
            dst_ref=held.at[group, item],
            send_sem=send_sem,
            recv_sem=x_recv.at[group, item],
            device_id={"section": sect, "tensor": tensor},
            device_id_type=MESH,
        )

    def forward_copy(way, group, item, tensor):
        return x_copy(
            held.at[group, item], group, item, section, tensor, x_send.at[way, group, item]
        )

    def relay_copy(group, item):
        return x_copy(
            sums_out.at[group, item], group, item + chunks, following, me,
            sum_send.at[group, item],
        )

    def sum_copy(way, group, item, tensor):
        return pltpu.make_async_remote_copy(
            src_ref=sums_out.at[group, item],
            dst_ref=sums_in.at[way, group, item],
            send_sem=sum_send.at[group, item],
            recv_sem=sum_recv.at[way, group, item],
            device_id={"section": section, "tensor": tensor},
            device_id_type=MESH,
        )

    def final_copy(src, send_sem, tick, piece, sect, home):
        return pltpu.make_async_remote_copy(
            src_ref=src,
            dst_ref=o_ref.at[tick, piece],
            send_sem=send_sem,
            recv_sem=final_recv.at[tick, piece],
            device_id={"section": sect, "tensor": home},
            device_id_type=MESH,
        )

    def pass_copy(group, item):
        return pltpu.make_async_remote_copy(
            src_ref=sums_out.at[group, item],
            dst_ref=passing.at[item],
            send_sem=sum_send.at[group, item],
            recv_sem=pass_recv.at[item],
            device_id={"section": following, "tensor": me},
            device_id_type=MESH,
        )

    places = (me, n - 1 - me)
    ahead = (me + 1, me - 1)
    back = (me - 1, me + 1)
    spread_lag = [
        jnp.where(at <= near, near - at, at - near) * hop_slots for at in places
    ]
    gather_lag = [
        jnp.where(at <= near, near + at, 2 * n - 2 - near - at) * hop_slots for at in places
    ]
    end_lag = (2 * n - 2 - near - far) * hop_slots

    def place(sect, side, item):
        tick, chunk = lax.div(item, chunks), lax.rem(item, chunks)
        shard, piece = lax.div(chunk, pieces), lax.rem(chunk, pieces)
        turns = jnp.minimum(tick, sect) + entry_side(sect - tick)
        group = lax.rem(turns + side, 2)
        home = jnp.where(group == 0, shard, n - 1 - shard)
        return tick, piece, home, group

    def enter(tick, piece, carry):
        item = tick * chunks + my_shard * pieces + piece
        source, start = x_ref.at[piece], my_start
        if tick:
            source, start = staged.at[tick - 1, piece], my_side
            staged[tick - 1, piece] = patches_ref[plan_ref[tick - 1], piece]
        if tick == 0:
            held[my_group, item] = source[...]
        else:

            @pl.when(section == 0)
            def _():
                held[my_group, item] = source[...]

        sends = me != start
        if tick:
            sends = sends & (section == carriers[tick - 1])

        @pl.when(sends)
        def _():
            sect = 0 if tick else section
            x_copy(source, my_group, item, sect, start, ship_send.at[tick, piece]).start()

        return carry

    lax.fori_loop(0, pieces, functools.partial(enter, 0), 0)

    @pl.when(carries)
    def _():
        loads[2].wait()
        for tick in range(1, TICKS):
            lax.fori_loop(0, pieces, functools.partial(enter, tick), 0)

    def at_slot(slot, lag):
        item = slot - lag
        return item, (item >= 0) & (item < items)

    def hands_on(side, entry, home):
        at = places[side]
        goes_back = (at > 0) & (at <= near) & jnp.logical_not(entry & (home == back[side]))
        goes_ahead = (
            (at >= near) & (at < n - 1) & jnp.logical_not(entry & (home == ahead[side]))
        )
        return goes_back, goes_ahead

    def receive(slot, side):
        item, active = at_slot(slot, spread_lag[side])

        @pl.when(active)
        def _():
            tick, piece, home, group = place(section, side, item)
            entry = (tick == 0) | (section == 0)

            @pl.when(jnp.logical_not(entry & (home == me)))
            def _():
                forward_copy(0, group, item, me).wait_recv()

            goes_back, goes_ahead = hands_on(side, entry, home)

            @pl.when(goes_ahead)
            def _():
                forward_copy(1, group, item, ahead[side]).start()

            @pl.when(goes_back)
            def _():
                forward_copy(0, group, item, back[side]).start()

            @pl.when((tick > 0) & (section > 0) & (home == me))
            def _():
                o_ref[tick - 1, piece] = held[group, item]

    def finish(slot, side):
        item, active = at_slot(slot, gather_lag[side])
        at = places[side]
        part = pl.ds(side * rows, rows)

        @pl.when(active)
        def _():
            tick, piece, home, group = place(section, side, item)

            @pl.when((at > 0) & (at <= far))
            def _():
                sum_copy(0, group, item, me).wait_recv()
                total[part] += sums_in[0, group, item].astype(jnp.float32)

            @pl.when((at >= far) & (at < n - 1))
            def _():
                sum_copy(1, group, item, me).wait_recv()
                total[part] += sums_in[1, group, item].astype(jnp.float32)

            @pl.when(at != far)
            def _():
                sums_out[group, item] = total[part].astype(jnp.bfloat16)

            @pl.when(at < far)
            def _():
                sum_copy(0, group, item, ahead[side]).start()

            @pl.when(at > far)
            def _():
                sum_copy(1, group, item, back[side]).start()

            @pl.when(at == far)
            def _():
                sums_out[group, item] = (
                    held[group, item].astype(jnp.float32) + total[part] + ob_ref[...]
                ).astype(jnp.bfloat16)
                leaves = (tick == TICKS - 1) | (following == 0)
                passes = (following == 0) & (home != me)

                @pl.when(passes)
                def _():
                    pass_copy(group, item).start()

                @pl.when(leaves & jnp.logical_not(passes))
                def _():
                    final_copy(
                        sums_out.at[group, item], sum_send.at[group, item],
                        tick, piece, following, home,
                    ).start()

                @pl.when(jnp.logical_not(leaves))
                def _():
                    relay_copy(group, item).start()

    def pass_on(slot, side, settled):
        item, active = at_slot(slot, end_lag + PASS_LAG)
        tick, piece, home, group = place(sections - 1, side, item)

        @pl.when(active & (section == 0) & (places[side] == far) & (home != me))
        def _():
            copy = final_copy(
                passing.at[item], pass_send.at[item], tick, piece, section, home
            )
            if settled:
                copy.wait_send()
            else:
                pass_copy(group, item).wait_recv()
                copy.start()

    def compute(slot):
        found = [at_slot(slot, lag) for lag in gather_lag]

        @pl.when(found[0][1] | found[1][1])
        def _():
            blocks = []
            for side in range(2):
                own, other = found[side], found[1 - side]
                group = jnp.where(
                    own[1],
                    place(section, side, own[0])[3],
                    place(section, 1 - side, other[0])[3],
                )
                blocks.append(held[group, jnp.where(own[1], own[0], other[0])])
            normed = normalize(
                jnp.concatenate(blocks, axis=0).astype(jnp.float32),
                gain_ref[...], shift_ref[...],
            )
            preact = lax.dot_general(
                normed, win_ref[...], (((1,), (1,)), ((), ())),
                preferred_element_type=jnp.float32,
            )
            hidden = activate(preact + ib_ref[...].astype(jnp.float32)).astype(jnp.bfloat16)
            total[...] = jnp.dot(hidden, wout_ref[...], preferred_element_type=jnp.float32)

        finish(slot, 0)
        finish(slot, 1)

    def settle(slot, side):
        item, active = at_slot(slot, spread_lag[side])

        @pl.when(active)
        def _():
            tick, piece, home, group = place(section, side, item)
            goes_back, goes_ahead = hands_on(side, (tick == 0) | (section == 0), home)

            @pl.when(goes_ahead)
            def _():
                forward_copy(1, group, item, me).wait_send()

            @pl.when(goes_back)
            def _():
                forward_copy(0, group, item, me).wait_send()

        summed, ready = at_slot(slot, gather_lag[side])

        @pl.when(ready)
        def _():
            group = place(section, side, summed)[3]
            sum_copy(0, group, summed, me).wait_send()

    def turn(slot, carry):
        compute(slot)
        for side in range(2):
            receive(slot + 1, side)
        for side in range(2):
            pass_on(slot, side, False)
        for side in range(2):
            settle(slot - SETTLE_LAG, side)
            pass_on(slot - SETTLE_LAG, side, True)
        return carry

    for side in range(2):
        receive(jnp.int32(0), side)
    for load in loads[:2]:
        load.wait()
    lax.fori_loop(0, items + end_lag + SETTLE_LAG + PASS_LAG, turn, 0)

    def unship(tick, piece, carry):
        start = my_side if tick else my_start
        sends = me != start
        if tick:
            sends = sends & (section == carriers[tick - 1])

        @pl.when(sends)
        def _():
            x_copy(
                staged.at[0, piece], 0, 0, section, me, ship_send.at[tick, piece]
            ).wait_send()

        return carry

    def collect(tick, piece, carry):
        final_copy(
            passing.at[0], pass_send.at[0], tick, piece, section, me
        ).wait_recv()
        return carry

    lax.fori_loop(0, pieces, functools.partial(unship, 0), 0)
    lax.fori_loop(0, pieces, functools.partial(collect, TICKS - 1), 0)

    @pl.when(carries)
    def _():
        for tick in range(1, TICKS):
            lax.fori_loop(0, pieces, functools.partial(unship, tick), 0)

    @pl.when(section == 0)
    def _():
        for tick in range(TICKS - 1):
            lax.fori_loop(0, pieces, functools.partial(collect, tick), 0)


def relay_call(n, sections, pieces, hop_slots, args):
    x, w_in, in_bias, w_out, out_bias, gain, shift, patches, plan = args
    tokens, width = x.shape
    rows = tokens // pieces
    items = TICKS * n // 2 * pieces
    micro = patches.shape[0]
    bf16 = jnp.bfloat16
    vmem = pl.BlockSpec(memory_space=pltpu.VMEM)
    hbm = pl.BlockSpec(memory_space=pl.ANY)
    every = (2, items, rows, width)
    dma = pltpu.SemaphoreType.DMA
    out = pl.pallas_call(
        functools.partial(relay_kernel, n, sections, hop_slots),
        out_shape=jax.ShapeDtypeStruct((TICKS, pieces, rows, width), bf16),
        in_specs=[vmem, hbm, vmem, hbm, vmem, vmem, vmem, hbm]
        + [pl.BlockSpec(memory_space=pltpu.SMEM)],
        out_specs=vmem,
        scratch_shapes=[
            pltpu.VMEM(w_in.shape, bf16),
            pltpu.VMEM(w_out.shape, bf16),
            pltpu.VMEM((micro, pieces, rows, width), bf16),
            dma((3,)),
            pltpu.VMEM(every, bf16),
            pltpu.VMEM((2,) + every, bf16),
            pltpu.VMEM(every, bf16),
            pltpu.VMEM((TICKS - 1, pieces, rows, width), bf16),
            pltpu.VMEM(every[1:], bf16),
            pltpu.VMEM((2 * rows, width), jnp.float32),
            dma((2, 2, items)),
            dma((2, items)),
            dma((2, items)),
            dma((2, 2, items)),
            dma((TICKS, pieces)),
            dma((items,)),
            dma((items,)),
            dma((TICKS, pieces)),
        ],
        compiler_params=pltpu.CompilerParams(
            collective_id=0, has_side_effects=True, vmem_limit_bytes=VMEM_BYTES
        ),
    )(
        x.reshape(pieces, rows, width),
        w_in,
        in_bias.reshape(1, -1),
        w_out,
        out_bias.reshape(1, -1),
        gain.reshape(1, -1),
        shift.reshape(1, -1),
        patches.reshape(micro, pieces, rows, width),
        plan,
    )
    return out.reshape(1, TICKS, tokens, width)


def passed_along(value, axis, steps):
    count = lax.axis_size(axis)
    pairs = [(source, (source + steps) % count) for source in range(count)]
    return lax.ppermute(value, axis, pairs)


def gathered_weights(args):
    current, w_in, in_bias, w_out, bias_row, gain_row, shift_row, patches, plan = args
    section_index = lax.axis_index("section")
    full_in, full_bias, full_out = (
        lax.all_gather(value, "tensor", axis=0, tiled=True) for value in (w_in, in_bias, w_out)
    )
    records = []
    for tick_index in range(TICKS):
        widened = current.astype(jnp.float32)
        normed = normalize(widened, gain_row, shift_row)
        preact = lax.dot_general(
            normed, full_in, (((1,), (1,)), ((), ())), preferred_element_type=jnp.float32
        )
        hidden = activate(preact + full_bias.astype(jnp.float32)).astype(jnp.bfloat16)
        produced = (
            widened + jnp.dot(hidden, full_out, preferred_element_type=jnp.float32) + bias_row
        ).astype(jnp.bfloat16)
        arrived = passed_along(produced, "section", 1)
        records.append(arrived)
        if tick_index + 1 < TICKS:
            selected = lax.dynamic_index_in_dim(patches, plan[tick_index], 0, keepdims=False)
            current = jnp.where(section_index == 0, selected, arrived)
    return jnp.stack(records, axis=0)[None]


def shards(n, sections, *blocks):
    args = tuple(block[0] for block in blocks[:7]) + blocks[7:]
    tokens, width = args[0].shape
    room = 2 * width * (
        tokens * (TICKS * (5 * n + 2) + 1 + args[7].shape[0]) + 2 * args[1].shape[0]
    )
    if tokens % (PIECES * 16) or n % 2 or sections < 2 or room > VMEM_BYTES * 3 // 4:
        return gathered_weights(args)
    return relay_call(n, sections, PIECES, HOP_SLOTS, args)


def solution(mesh):
    placed = (
        P("section", "tensor", None),
        P("section", "tensor", None),
        P("section", "tensor"),
        P("section", "tensor", None),
        P("section", None),
        P("section", None),
        P("section", None),
        P(None, "tensor", None),
        P(),
    )
    return jax.shard_map(
        functools.partial(shards, mesh.shape["tensor"], mesh.shape["section"]),
        mesh=mesh,
        in_specs=placed,
        out_specs=P("section", None, "tensor", None),
        check_vma=False,
    )
```

time: 123 us -> 116 us (0.943)
  Pallas kernels: 120 us -> 114 us
    pallas_call x1, Pallas kernels: 120 us -> 114 us  [relay_call(): pl.pallas_call(functools.partial(relay_kernel, n, sections, hop_slots), o...]
where the time goes in v1:
time: 116 us
  Pallas kernels  114 us (98%)
  local copies, waits for them, and re-layouts  2.26 us (2%)
    pallas_call x1, Pallas kernels, relay_call(): pl.pallas_call(functools.partial(relay_kernel, n, sections, hop_slots), o...  114 us

profile of v1, /device:TPU:17, one launch (start us, length us, event | category | flops | bytes accessed | tf_op | source)
XLA Modules:
  0.0 115.9 jit_solution(12966836624607437079)
XLA Ops:
  0.0 113.7 %shard_map.91 = bf16[4,4,32,1024]{3,2,1,0:T(8,128)(2,1)} custom-call(bf16[4,32,1024]{2,1,0:T(8,128)(2,1)} %bitcast.9, bf16[576,1024]{1,0:T(8,128)(2,1)} %bitcast.7, bf16[1,576]{1,0:T(2,128)(2,1)} %ib_ref.1, bf16[576,1024]{1,0:T(8,128)(2,1)} %bitcast.8, f32[1,1024]{1,0:T(1,128)} %ob_ref.1, f32[1,1024]{1,0:T(1,128)} %gain_ref.1, f32[1,1024]{1,0:T(1,128)} %shift_ref.1, ...), custom_call_target="tpu_custom_call" | custom-call | tf_op jit(solution)/shard_map/pallas_call | solution.py:430
  113.7 2.3 %copy.11 = bf16[1,4,128,1024]{3,2,1,0:T(8,128)(2,1)} copy(bf16[1,4,128,1024]{3,2,1,0:T(8,128)(2,1)} %bitcast.5) | data formatting | bytes 2097152

commit v2 on v1

--- a/solution.py
+++ b/solution.py
@@ -34,12 +34,13 @@
 
 def relay_kernel(
     n, sections, hop_slots,
-    x_ref, win_hbm, ib_ref, wout_hbm, ob_ref, gain_ref, shift_ref, patches_hbm, plan_ref,
+    x_hbm, win_hbm, ib_hbm, wout_hbm, ob_hbm, gain_hbm, shift_hbm, patches_hbm, plan_hbm,
     o_ref,
-    win_ref, wout_ref, patches_ref, load_sem, held, sums_in, sums_out, staged, passing, total,
+    x_ref, win_ref, ib_ref, wout_ref, ob_ref, gain_ref, shift_ref, patches_ref, plan_ref,
+    load_sem, held, sums_in, sums_out, staged, passing, total,
     x_send, x_recv, sum_send, sum_recv, ship_send, pass_send, pass_recv, final_recv,
 ):
-    pieces, rows = x_ref.shape[0], x_ref.shape[1]
+    pieces, rows = x_hbm.shape[0], x_hbm.shape[1]
     near, far = n // 2 - 1, n // 2
     chunks = n // 2 * pieces
     items = TICKS * chunks
@@ -52,16 +53,6 @@
     carries = section == 0
     for carrier in carriers:
         carries = carries | (section == carrier)
-
-    loads = [
-        pltpu.make_async_copy(source, target, load_sem.at[index])
-        for index, (source, target) in enumerate(
-            [(win_hbm, win_ref), (wout_hbm, wout_ref), (patches_hbm, patches_ref)]
-        )
-    ]
-    for load in loads[:2]:
-        load.start()
-    pl.when(carries)(loads[2].start)
 
     def entry_side(origin):
         length = jnp.minimum(TICKS, sections - origin)
@@ -97,6 +88,24 @@
                 pl.when((section == 0) & (me == (near, far)[group]))(
                     functools.partial(greet, carrier, home)
                 )
+    loads = [
+        pltpu.make_async_copy(source, target, load_sem.at[index])
+        for index, (source, target) in enumerate(
+            [
+                (x_hbm, x_ref), (gain_hbm, gain_ref), (shift_hbm, shift_ref),
+                (win_hbm, win_ref), (ib_hbm, ib_ref), (wout_hbm, wout_ref),
+                (ob_hbm, ob_ref), (plan_hbm, plan_ref), (patches_hbm, patches_ref),
+            ]
+        )
+    ]
+    for load in loads[:7]:
+        load.start()
+
+    @pl.when(carries)
+    def _():
+        for load in loads[7:]:
+            load.start()
+
     expected = 4 - jnp.where((me == 0) | (me == n - 1), 1, 0)
     expected = expected + jnp.where(jnp.abs(me - my_start) > 1, 1, 0)
     for carrier in carriers:
@@ -199,11 +208,13 @@
 
         return carry
 
+    loads[0].wait()
     lax.fori_loop(0, pieces, functools.partial(enter, 0), 0)
 
     @pl.when(carries)
     def _():
-        loads[2].wait()
+        for load in loads[7:]:
+            load.wait()
         for tick in range(1, TICKS):
             lax.fori_loop(0, pieces, functools.partial(enter, tick), 0)
 
@@ -282,7 +293,7 @@
                     held[group, item].astype(jnp.float32) + total[part] + ob_ref[...]
                 ).astype(jnp.bfloat16)
                 leaves = (tick == TICKS - 1) | (following == 0)
-                passes = (following == 0) & (home != me)
+                passes = (following == 0) & (home != me) & (tick < TICKS - 1)
 
                 @pl.when(passes)
                 def _():
@@ -303,7 +314,9 @@
         item, active = at_slot(slot, end_lag + PASS_LAG)
         tick, piece, home, group = place(sections - 1, side, item)
 
-        @pl.when(active & (section == 0) & (places[side] == far) & (home != me))
+        @pl.when(
+            active & (section == 0) & (places[side] == far) & (home != me) & (tick < TICKS - 1)
+        )
         def _():
             copy = final_copy(
                 passing.at[item], pass_send.at[item], tick, piece, section, home
@@ -378,7 +391,7 @@
 
     for side in range(2):
         receive(jnp.int32(0), side)
-    for load in loads[:2]:
+    for load in loads[1:7]:
         load.wait()
     lax.fori_loop(0, items + end_lag + SETTLE_LAG + PASS_LAG, turn, 0)
 
@@ -424,20 +437,24 @@
     micro = patches.shape[0]
     bf16 = jnp.bfloat16
     vmem = pl.BlockSpec(memory_space=pltpu.VMEM)
-    hbm = pl.BlockSpec(memory_space=pl.ANY)
     every = (2, items, rows, width)
     dma = pltpu.SemaphoreType.DMA
     out = pl.pallas_call(
         functools.partial(relay_kernel, n, sections, hop_slots),
-        out_shape=jax.ShapeDtypeStruct((TICKS, pieces, rows, width), bf16),
-        in_specs=[vmem, hbm, vmem, hbm, vmem, vmem, vmem, hbm]
-        + [pl.BlockSpec(memory_space=pltpu.SMEM)],
+        out_shape=pltpu.VMEM((TICKS, pieces, rows, width), bf16),
+        in_specs=[pl.BlockSpec(memory_space=pl.ANY)] * 9,
         out_specs=vmem,
         scratch_shapes=[
+            pltpu.VMEM((pieces, rows, width), bf16),
             pltpu.VMEM(w_in.shape, bf16),
+            pltpu.VMEM((1, w_in.shape[0]), bf16),
             pltpu.VMEM(w_out.shape, bf16),
+            pltpu.VMEM((1, width), jnp.float32),
+            pltpu.VMEM((1, width), jnp.float32),
+            pltpu.VMEM((1, width), jnp.float32),
             pltpu.VMEM((micro, pieces, rows, width), bf16),
-            dma((3,)),
+            pltpu.SMEM(plan.shape, jnp.int32),
+            dma((9,)),
             pltpu.VMEM(every, bf16),
             pltpu.VMEM((2,) + every, bf16),
             pltpu.VMEM(every, bf16),

time: 116 us -> 113 us (0.974)
  Pallas kernels: 114 us -> 111 us
  local copies, waits for them, and re-layouts: 2.26 us -> 0.97 us
    pallas_call x1, Pallas kernels: 114 us -> 111 us  [relay_call(): pl.pallas_call(functools.partial(relay_kernel, n, sections, hop_slots), o...]
    unnamed x1, local copies, waits for them, and re-layouts: 2.26 us -> 0.97 us
where the time goes in v2:
time: 113 us; the launch traced here: 112 us
  Pallas kernels  111 us (98%)
    pallas_call x1, Pallas kernels, relay_call(): pl.pallas_call(functools.partial(relay_kernel, n, sections, hop_slots), o...  111 us

profile of v2, /device:TPU:17, one launch (start us, length us, event | category | flops | bytes accessed | tf_op | source)
XLA Modules:
  0.0 112.4 jit_solution(17236144089610706247)
XLA Ops:
  0.0 111.5 %shard_map.91 = bf16[4,4,32,1024]{3,2,1,0:T(8,128)(2,1)S(1)} custom-call(bf16[4,32,1024]{2,1,0:T(8,128)(2,1)} %bitcast.9, bf16[576,1024]{1,0:T(8,128)(2,1)} %bitcast.7, bf16[1,576]{1,0:T(2,128)(2,1)} %ib_hbm.1, bf16[576,1024]{1,0:T(8,128)(2,1)} %bitcast.8, f32[1,1024]{1,0:T(1,128)} %ob_hbm.1, f32[1,1024]{1,0:T(1,128)} %gain_hbm.1, f32[1,1024]{1,0:T(1,128)} %shift_hbm.1, ...), custom_call_target="tpu_custom_call" | custom-call | tf_op jit(solution)/shard_map/pallas_call | solution.py:442
  111.5 1.0 copy.11

commit v3 on v2

--- a/solution.py
+++ b/solution.py
@@ -11,6 +11,7 @@
 PIECES = 4
 HOP_SLOTS = 2
 SETTLE_LAG = 3
+SEND_RING = 4
 PASS_LAG = 2
 VMEM_BYTES = 60 * 1024 * 1024
 
@@ -38,7 +39,7 @@
     o_ref,
     x_ref, win_ref, ib_ref, wout_ref, ob_ref, gain_ref, shift_ref, patches_ref, plan_ref,
     load_sem, held, sums_in, sums_out, staged, passing, total,
-    x_send, x_recv, sum_send, sum_recv, ship_send, pass_send, pass_recv, final_recv,
+    x_send, x_recv, relay_recv, sum_send, sum_recv, ship_send, pass_send, pass_recv, final_recv,
 ):
     pieces, rows = x_hbm.shape[0], x_hbm.shape[1]
     near, far = n // 2 - 1, n // 2
@@ -113,33 +114,40 @@
             expected = expected + jnp.where((section == carrier) & (me != my_side), 1, 0)
     pl.semaphore_wait(barrier, expected)
 
-    def x_copy(src, group, item, sect, tensor, send_sem):
+    def x_copy(src, group, item, sect, tensor, send_sem, recv_sem):
         return pltpu.make_async_remote_copy(
             src_ref=src,
             dst_ref=held.at[group, item],
             send_sem=send_sem,
-            recv_sem=x_recv.at[group, item],
+            recv_sem=recv_sem,
             device_id={"section": sect, "tensor": tensor},
             device_id_type=MESH,
         )
 
-    def forward_copy(way, group, item, tensor):
+    def spread_sem(group, item):
+        return x_recv.at[group, lax.rem(item, chunks)]
+
+    def forward_copy(way, side, group, item, tensor):
         return x_copy(
-            held.at[group, item], group, item, section, tensor, x_send.at[way, group, item]
-        )
-
-    def relay_copy(group, item):
+            held.at[group, item], group, item, section, tensor,
+            x_send.at[way, side, lax.rem(item, SEND_RING)], spread_sem(group, item),
+        )
+
+    def outgoing(side, item):
+        return sum_send.at[side, lax.rem(item, SEND_RING)]
+
+    def relay_copy(side, group, item):
         return x_copy(
             sums_out.at[group, item], group, item + chunks, following, me,
-            sum_send.at[group, item],
-        )
-
-    def sum_copy(way, group, item, tensor):
+            outgoing(side, item), relay_recv.at[item],
+        )
+
+    def sum_copy(way, side, group, item, tensor):
         return pltpu.make_async_remote_copy(
             src_ref=sums_out.at[group, item],
             dst_ref=sums_in.at[way, group, item],
-            send_sem=sum_send.at[group, item],
-            recv_sem=sum_recv.at[way, group, item],
+            send_sem=outgoing(side, item),
+            recv_sem=sum_recv.at[way, group, lax.rem(item, chunks)],
             device_id={"section": section, "tensor": tensor},
             device_id_type=MESH,
         )
@@ -154,12 +162,12 @@
             device_id_type=MESH,
         )
 
-    def pass_copy(group, item):
+    def pass_copy(side, group, item, tick, piece):
         return pltpu.make_async_remote_copy(
             src_ref=sums_out.at[group, item],
-            dst_ref=passing.at[item],
-            send_sem=sum_send.at[group, item],
-            recv_sem=pass_recv.at[item],
+            dst_ref=passing.at[tick, piece],
+            send_sem=outgoing(side, item),
+            recv_sem=pass_recv.at[tick, piece],
             device_id={"section": following, "tensor": me},
             device_id_type=MESH,
         )
@@ -204,7 +212,10 @@
         @pl.when(sends)
         def _():
             sect = 0 if tick else section
-            x_copy(source, my_group, item, sect, start, ship_send.at[tick, piece]).start()
+            arrival = relay_recv.at[item - chunks] if tick else spread_sem(my_group, item)
+            x_copy(
+                source, my_group, item, sect, start, ship_send.at[tick, piece], arrival
+            ).start()
 
         return carry
 
@@ -238,19 +249,26 @@
             tick, piece, home, group = place(section, side, item)
             entry = (tick == 0) | (section == 0)
 
-            @pl.when(jnp.logical_not(entry & (home == me)))
-            def _():
-                forward_copy(0, group, item, me).wait_recv()
+            arrives = jnp.logical_not(entry & (home == me))
+            starts = (places[side] == near) & (tick > 0)
+
+            @pl.when(arrives & starts)
+            def _():
+                relay_copy(side, group, item - chunks).wait_recv()
+
+            @pl.when(arrives & jnp.logical_not(starts))
+            def _():
+                forward_copy(0, side, group, item, me).wait_recv()
 
             goes_back, goes_ahead = hands_on(side, entry, home)
 
             @pl.when(goes_ahead)
             def _():
-                forward_copy(1, group, item, ahead[side]).start()
+                forward_copy(1, side, group, item, ahead[side]).start()
 
             @pl.when(goes_back)
             def _():
-                forward_copy(0, group, item, back[side]).start()
+                forward_copy(0, side, group, item, back[side]).start()
 
             @pl.when((tick > 0) & (section > 0) & (home == me))
             def _():
@@ -267,12 +285,12 @@
 
             @pl.when((at > 0) & (at <= far))
             def _():
-                sum_copy(0, group, item, me).wait_recv()
+                sum_copy(0, side, group, item, me).wait_recv()
                 total[part] += sums_in[0, group, item].astype(jnp.float32)
 
             @pl.when((at >= far) & (at < n - 1))
             def _():
-                sum_copy(1, group, item, me).wait_recv()
+                sum_copy(1, side, group, item, me).wait_recv()
                 total[part] += sums_in[1, group, item].astype(jnp.float32)
 
             @pl.when(at != far)
@@ -281,11 +299,11 @@
 
             @pl.when(at < far)
             def _():
-                sum_copy(0, group, item, ahead[side]).start()
+                sum_copy(0, side, group, item, ahead[side]).start()
 
             @pl.when(at > far)
             def _():
-                sum_copy(1, group, item, back[side]).start()
+                sum_copy(1, side, group, item, back[side]).start()
 
             @pl.when(at == far)
             def _():
@@ -297,18 +315,18 @@
 
                 @pl.when(passes)
                 def _():
-                    pass_copy(group, item).start()
+                    pass_copy(side, group, item, tick, piece).start()
 
                 @pl.when(leaves & jnp.logical_not(passes))
                 def _():
                     final_copy(
-                        sums_out.at[group, item], sum_send.at[group, item],
+                        sums_out.at[group, item], outgoing(side, item),
                         tick, piece, following, home,
                     ).start()
 
                 @pl.when(jnp.logical_not(leaves))
                 def _():
-                    relay_copy(group, item).start()
+                    relay_copy(side, group, item).start()
 
     def pass_on(slot, side, settled):
         item, active = at_slot(slot, end_lag + PASS_LAG)
@@ -319,12 +337,12 @@
         )
         def _():
             copy = final_copy(
-                passing.at[item], pass_send.at[item], tick, piece, section, home
+                passing.at[tick, piece], pass_send.at[piece], tick, piece, section, home
             )
             if settled:
                 copy.wait_send()
             else:
-                pass_copy(group, item).wait_recv()
+                pass_copy(side, group, item, tick, piece).wait_recv()
                 copy.start()
 
     def compute(slot):
@@ -365,28 +383,26 @@
 
             @pl.when(goes_ahead)
             def _():
-                forward_copy(1, group, item, me).wait_send()
+                forward_copy(1, side, group, item, me).wait_send()
 
             @pl.when(goes_back)
             def _():
-                forward_copy(0, group, item, me).wait_send()
+                forward_copy(0, side, group, item, me).wait_send()
 
         summed, ready = at_slot(slot, gather_lag[side])
 
         @pl.when(ready)
         def _():
-            group = place(section, side, summed)[3]
-            sum_copy(0, group, summed, me).wait_send()
+            sum_copy(0, side, 0, summed, me).wait_send()
 
     def turn(slot, carry):
         compute(slot)
         for side in range(2):
+            settle(slot - SETTLE_LAG, side)
             receive(slot + 1, side)
         for side in range(2):
+            pass_on(slot - SETTLE_LAG, side, True)
             pass_on(slot, side, False)
-        for side in range(2):
-            settle(slot - SETTLE_LAG, side)
-            pass_on(slot - SETTLE_LAG, side, True)
         return carry
 
     for side in range(2):
@@ -404,14 +420,15 @@
         @pl.when(sends)
         def _():
             x_copy(
-                staged.at[0, piece], 0, 0, section, me, ship_send.at[tick, piece]
+                staged.at[0, piece], 0, 0, section, me, ship_send.at[tick, piece],
+                spread_sem(0, 0),
             ).wait_send()
 
         return carry
 
     def collect(tick, piece, carry):
         final_copy(
-            passing.at[0], pass_send.at[0], tick, piece, section, me
+            passing.at[0, 0], pass_send.at[0], tick, piece, section, me
         ).wait_recv()
         return carry
 
@@ -433,7 +450,8 @@
     x, w_in, in_bias, w_out, out_bias, gain, shift, patches, plan = args
     tokens, width = x.shape
     rows = tokens // pieces
-    items = TICKS * n // 2 * pieces
+    chunks = n // 2 * pieces
+    items = TICKS * chunks
     micro = patches.shape[0]
     bf16 = jnp.bfloat16
     vmem = pl.BlockSpec(memory_space=pltpu.VMEM)
@@ -459,15 +477,16 @@
             pltpu.VMEM((2,) + every, bf16),
             pltpu.VMEM(every, bf16),
             pltpu.VMEM((TICKS - 1, pieces, rows, width), bf16),
-            pltpu.VMEM(every[1:], bf16),
+            pltpu.VMEM((TICKS - 1, pieces, rows, width), bf16),
             pltpu.VMEM((2 * rows, width), jnp.float32),
-            dma((2, 2, items)),
-            dma((2, items)),
-            dma((2, items)),
-            dma((2, 2, items)),
+            dma((2, 2, SEND_RING)),
+            dma((2, chunks)),
+            dma((items - chunks,)),
+            dma((2, SEND_RING)),
+            dma((2, 2, chunks)),
             dma((TICKS, pieces)),
-            dma((items,)),
-            dma((items,)),
+            dma((pieces,)),
+            dma((TICKS - 1, pieces)),
             dma((TICKS, pieces)),
         ],
         compiler_params=pltpu.CompilerParams(

time: 113 us -> 110 us (0.973)
  Pallas kernels: 111 us -> 108 us
    pallas_call x1, Pallas kernels: 111 us -> 108 us  [relay_call(): pl.pallas_call(functools.partial(relay_kernel, n, sections, hop_slots), o...]
where the time goes in v3:
time: 110 us; the launch traced here: 109 us
  Pallas kernels  108 us (98%)
    pallas_call x1, Pallas kernels, relay_call(): pl.pallas_call(functools.partial(relay_kernel, n, sections, hop_slots), o...  108 us

profile of v3, /device:TPU:17, one launch (start us, length us, event | category | flops | bytes accessed | tf_op | source)
XLA Modules:
  0.0 109.4 jit_solution(1450546772344596274)
XLA Ops:
  0.0 108.4 %shard_map.91 = bf16[4,4,32,1024]{3,2,1,0:T(8,128)(2,1)S(1)} custom-call(bf16[4,32,1024]{2,1,0:T(8,128)(2,1)} %bitcast.9, bf16[576,1024]{1,0:T(8,128)(2,1)} %bitcast.7, bf16[1,576]{1,0:T(2,128)(2,1)} %ib_hbm.1, bf16[576,1024]{1,0:T(8,128)(2,1)} %bitcast.8, f32[1,1024]{1,0:T(1,128)} %ob_hbm.1, f32[1,1024]{1,0:T(1,128)} %gain_hbm.1, f32[1,1024]{1,0:T(1,128)} %shift_hbm.1, ...), custom_call_target="tpu_custom_call" | custom-call | tf_op jit(solution)/shard_map/pallas_call | solution.py:460
  108.5 1.0 copy.11

commit v4 on v3

--- a/solution.py
+++ b/solution.py
@@ -157,7 +157,7 @@
             src_ref=src,
             dst_ref=o_ref.at[tick, piece],
             send_sem=send_sem,
-            recv_sem=final_recv.at[tick, piece],
+            recv_sem=final_recv.at[tick],
             device_id={"section": sect, "tensor": home},
             device_id_type=MESH,
         )
@@ -214,7 +214,7 @@
             sect = 0 if tick else section
             arrival = relay_recv.at[item - chunks] if tick else spread_sem(my_group, item)
             x_copy(
-                source, my_group, item, sect, start, ship_send.at[tick, piece], arrival
+                source, my_group, item, sect, start, ship_send.at[tick], arrival
             ).start()
 
         return carry
@@ -411,39 +411,44 @@
         load.wait()
     lax.fori_loop(0, items + end_lag + SETTLE_LAG + PASS_LAG, turn, 0)
 
-    def unship(tick, piece, carry):
-        start = my_side if tick else my_start
-        sends = me != start
+    def unship(tick):
+        sends = me != (my_side if tick else my_start)
         if tick:
             sends = sends & (section == carriers[tick - 1])
 
         @pl.when(sends)
         def _():
-            x_copy(
-                staged.at[0, piece], 0, 0, section, me, ship_send.at[tick, piece],
-                spread_sem(0, 0),
+            pltpu.make_async_remote_copy(
+                src_ref=x_ref,
+                dst_ref=o_ref.at[0],
+                send_sem=ship_send.at[tick],
+                recv_sem=final_recv.at[0],
+                device_id={"section": section, "tensor": me},
+                device_id_type=MESH,
             ).wait_send()
 
-        return carry
-
-    def collect(tick, piece, carry):
-        final_copy(
-            passing.at[0, 0], pass_send.at[0], tick, piece, section, me
+    def collect(tick):
+        pltpu.make_async_remote_copy(
+            src_ref=x_ref,
+            dst_ref=o_ref.at[tick],
+            send_sem=ship_send.at[0],
+            recv_sem=final_recv.at[tick],
+            device_id={"section": section, "tensor": me},
+            device_id_type=MESH,
         ).wait_recv()
-        return carry
-
-    lax.fori_loop(0, pieces, functools.partial(unship, 0), 0)
-    lax.fori_loop(0, pieces, functools.partial(collect, TICKS - 1), 0)
+
+    unship(0)
+    collect(TICKS - 1)
 
     @pl.when(carries)
     def _():
         for tick in range(1, TICKS):
-            lax.fori_loop(0, pieces, functools.partial(unship, tick), 0)
+            unship(tick)
 
     @pl.when(section == 0)
     def _():
         for tick in range(TICKS - 1):
-            lax.fori_loop(0, pieces, functools.partial(collect, tick), 0)
+            collect(tick)
 
 
 def relay_call(n, sections, pieces, hop_slots, args):
@@ -484,10 +489,10 @@
             dma((items - chunks,)),
             dma((2, SEND_RING)),
             dma((2, 2, chunks)),
-            dma((TICKS, pieces)),
+            dma((TICKS,)),
             dma((pieces,)),
             dma((TICKS - 1, pieces)),
-            dma((TICKS, pieces)),
+            dma((TICKS,)),
         ],
         compiler_params=pltpu.CompilerParams(
             collective_id=0, has_side_effects=True, vmem_limit_bytes=VMEM_BYTES

time: 110 us -> 110 us (level)
  no operation moved by 1% of the time
where the time goes in v4:
time: 110 us; the launch traced here: 109 us
  Pallas kernels  108 us (98%)
    pallas_call x1, Pallas kernels, relay_call(): pl.pallas_call(functools.partial(relay_kernel, n, sections, hop_slots), o...  108 us

profile of v4, /device:TPU:17, one launch (start us, length us, event | category | flops | bytes accessed | tf_op | source)
XLA Modules:
  0.0 109.2 jit_solution(8808674522947054848)
XLA Ops:
  0.0 108.2 %shard_map.91 = bf16[4,4,32,1024]{3,2,1,0:T(8,128)(2,1)S(1)} custom-call(bf16[4,32,1024]{2,1,0:T(8,128)(2,1)} %bitcast.9, bf16[576,1024]{1,0:T(8,128)(2,1)} %bitcast.7, bf16[1,576]{1,0:T(2,128)(2,1)} %ib_hbm.1, bf16[576,1024]{1,0:T(8,128)(2,1)} %bitcast.8, f32[1,1024]{1,0:T(1,128)} %ob_hbm.1, f32[1,1024]{1,0:T(1,128)} %gain_hbm.1, f32[1,1024]{1,0:T(1,128)} %shift_hbm.1, ...), custom_call_target="tpu_custom_call" | custom-call | tf_op jit(solution)/shard_map/pallas_call | solution.py:465
  108.2 1.0 copy.11

commit v5 on v4

--- a/solution.py
+++ b/solution.py
@@ -12,7 +12,7 @@
 HOP_SLOTS = 2
 SETTLE_LAG = 3
 SEND_RING = 4
-PASS_LAG = 2
+PASS_LAG = 1
 VMEM_BYTES = 60 * 1024 * 1024
 
 norm_floor = 0.1
@@ -49,7 +49,7 @@
     section = lax.axis_index("section")
     following = lax.rem(section + 1, sections)
     preceding = lax.rem(section + sections - 1, sections)
-    carriers = [2 * tick % sections for tick in range(1, TICKS)]
+    carriers = [(2 * tick + 1) % sections for tick in range(1, TICKS)]
 
     carries = section == 0
     for carrier in carriers:

time: 110 us -> 109 us (level)
  no operation moved by 1% of the time
where the time goes in v5:
time: 109 us
  Pallas kernels  108 us (99%)
    pallas_call x1, Pallas kernels, relay_call(): pl.pallas_call(functools.partial(relay_kernel, n, sections, hop_slots), o...  108 us

profile of v5, /device:TPU:17, one launch (start us, length us, event | category | flops | bytes accessed | tf_op | source)
XLA Modules:
  0.0 109.2 jit_solution(16325758093130226873)
XLA Ops:
  0.0 108.2 %shard_map.91 = bf16[4,4,32,1024]{3,2,1,0:T(8,128)(2,1)S(1)} custom-call(bf16[4,32,1024]{2,1,0:T(8,128)(2,1)} %bitcast.9, bf16[576,1024]{1,0:T(8,128)(2,1)} %bitcast.7, bf16[1,576]{1,0:T(2,128)(2,1)} %ib_hbm.1, bf16[576,1024]{1,0:T(8,128)(2,1)} %bitcast.8, f32[1,1024]{1,0:T(1,128)} %ob_hbm.1, f32[1,1024]{1,0:T(1,128)} %gain_hbm.1, f32[1,1024]{1,0:T(1,128)} %shift_hbm.1, ...), custom_call_target="tpu_custom_call" | custom-call | tf_op jit(solution)/shard_map/pallas_call | solution.py:465
  108.2 1.0 copy.11

commit v6 on v5

--- a/solution.py
+++ b/solution.py
@@ -38,8 +38,8 @@
     x_hbm, win_hbm, ib_hbm, wout_hbm, ob_hbm, gain_hbm, shift_hbm, patches_hbm, plan_hbm,
     o_ref,
     x_ref, win_ref, ib_ref, wout_ref, ob_ref, gain_ref, shift_ref, patches_ref, plan_ref,
-    load_sem, held, sums_in, sums_out, staged, passing, total,
-    x_send, x_recv, relay_recv, sum_send, sum_recv, ship_send, pass_send, pass_recv, final_recv,
+    load_sem, held, sums_in, sums_out, staged, passing, kept, total,
+    x_send, x_recv, relay_recv, sum_send, sum_recv, ship_send, pass_send, home_send, pass_recv, final_recv,
 ):
     pieces, rows = x_hbm.shape[0], x_hbm.shape[1]
     near, far = n // 2 - 1, n // 2
@@ -288,24 +288,32 @@
                 sum_copy(0, side, group, item, me).wait_recv()
                 total[part] += sums_in[0, group, item].astype(jnp.float32)
 
-            @pl.when((at >= far) & (at < n - 1))
+            homing = (tick == TICKS - 1) & (jnp.int32(far + 1) == n - 1)
+            turning = homing & (at == far) & (home == ahead[side])
+            ending = homing & (at == n - 1) & (home == me)
+
+            @pl.when((at >= far) & (at < n - 1) & jnp.logical_not(turning))
             def _():
                 sum_copy(1, side, group, item, me).wait_recv()
                 total[part] += sums_in[1, group, item].astype(jnp.float32)
 
-            @pl.when(at != far)
+            @pl.when(ending)
+            def _():
+                kept[piece] = held[group, item].astype(jnp.float32) + total[part] + ob_ref[...]
+
+            @pl.when(((at != far) | turning) & jnp.logical_not(ending))
             def _():
                 sums_out[group, item] = total[part].astype(jnp.bfloat16)
 
-            @pl.when(at < far)
+            @pl.when((at < far) | turning)
             def _():
                 sum_copy(0, side, group, item, ahead[side]).start()
 
-            @pl.when(at > far)
+            @pl.when((at > far) & jnp.logical_not(ending))
             def _():
                 sum_copy(1, side, group, item, back[side]).start()
 
-            @pl.when(at == far)
+            @pl.when((at == far) & jnp.logical_not(turning))
             def _():
                 sums_out[group, item] = (
                     held[group, item].astype(jnp.float32) + total[part] + ob_ref[...]
@@ -327,6 +335,21 @@
                 @pl.when(jnp.logical_not(leaves))
                 def _():
                     relay_copy(side, group, item).start()
+
+    def end_home(slot, side):
+        item, active = at_slot(slot, end_lag + hop_slots)
+        tick, piece, home, group = place(section, side, item)
+        last = (tick == TICKS - 1) & (jnp.int32(far + 1) == n - 1)
+
+        @pl.when(active & last & (places[side] == n - 1) & (home == me))
+        def _():
+            sum_copy(0, side, group, item, me).wait_recv()
+            sums_out[group, item] = (
+                kept[piece] + sums_in[0, group, item].astype(jnp.float32)
+            ).astype(jnp.bfloat16)
+            final_copy(
+                sums_out.at[group, item], home_send, tick, piece, following, me
+            ).start()
 
     def pass_on(slot, side, settled):
         item, active = at_slot(slot, end_lag + PASS_LAG)
@@ -370,9 +393,6 @@
             hidden = activate(preact + ib_ref[...].astype(jnp.float32)).astype(jnp.bfloat16)
             total[...] = jnp.dot(hidden, wout_ref[...], preferred_element_type=jnp.float32)
 
-        finish(slot, 0)
-        finish(slot, 1)
-
     def settle(slot, side):
         item, active = at_slot(slot, spread_lag[side])
 
@@ -393,13 +413,24 @@
 
         @pl.when(ready)
         def _():
-            sum_copy(0, side, 0, summed, me).wait_send()
+            tick, _, home, _ = place(section, side, summed)
+            ending = (
+                (tick == TICKS - 1) & (jnp.int32(far + 1) == n - 1)
+                & (places[side] == n - 1) & (home == me)
+            )
+
+            @pl.when(jnp.logical_not(ending))
+            def _():
+                sum_copy(0, side, 0, summed, me).wait_send()
 
     def turn(slot, carry):
         compute(slot)
         for side in range(2):
+            finish(slot, side)
             settle(slot - SETTLE_LAG, side)
             receive(slot + 1, side)
+        for side in range(2):
+            end_home(slot, side)
         for side in range(2):
             pass_on(slot - SETTLE_LAG, side, True)
             pass_on(slot, side, False)
@@ -426,6 +457,20 @@
                 device_id={"section": section, "tensor": me},
                 device_id_type=MESH,
             ).wait_send()
+
+    last_turns = jnp.minimum(TICKS - 1, section) + entry_side(section - TICKS + 1)
+    my_end = lax.rem(my_group + last_turns, 2)
+
+    @pl.when((jnp.int32(far + 1) == n - 1) & (jnp.where(my_end == 0, me, n - 1 - me) == n - 1))
+    def _():
+        pltpu.make_async_remote_copy(
+            src_ref=x_ref,
+            dst_ref=o_ref.at[0],
+            send_sem=home_send,
+            recv_sem=final_recv.at[0],
+            device_id={"section": section, "tensor": me},
+            device_id_type=MESH,
+        ).wait_send()
 
     def collect(tick):
         pltpu.make_async_remote_copy(
@@ -483,6 +528,7 @@
             pltpu.VMEM(every, bf16),
             pltpu.VMEM((TICKS - 1, pieces, rows, width), bf16),
             pltpu.VMEM((TICKS - 1, pieces, rows, width), bf16),
+            pltpu.VMEM((pieces, rows, width), jnp.float32),
             pltpu.VMEM((2 * rows, width), jnp.float32),
             dma((2, 2, SEND_RING)),
             dma((2, chunks)),
@@ -491,6 +537,7 @@
             dma((2, 2, chunks)),
             dma((TICKS,)),
             dma((pieces,)),
+            dma,
             dma((TICKS - 1, pieces)),
             dma((TICKS,)),
         ],

time: 109 us -> 109 us (level)
  no operation moved by 1% of the time
where the time goes in v6:
time: 109 us
  Pallas kernels  108 us (99%)
    pallas_call x1, Pallas kernels, relay_call(): pl.pallas_call(functools.partial(relay_kernel, n, sections, hop_slots), o...  108 us

profile of v6, /device:TPU:17, one launch (start us, length us, event | category | flops | bytes accessed | tf_op | source)
XLA Modules:
  0.0 109.2 jit_solution(5040924288194912149)
XLA Ops:
  0.0 108.2 %shard_map.91 = bf16[4,4,32,1024]{3,2,1,0:T(8,128)(2,1)S(1)} custom-call(bf16[4,32,1024]{2,1,0:T(8,128)(2,1)} %bitcast.9, bf16[576,1024]{1,0:T(8,128)(2,1)} %bitcast.7, bf16[1,576]{1,0:T(2,128)(2,1)} %ib_hbm.1, bf16[576,1024]{1,0:T(8,128)(2,1)} %bitcast.8, f32[1,1024]{1,0:T(1,128)} %ob_hbm.1, f32[1,1024]{1,0:T(1,128)} %gain_hbm.1, f32[1,1024]{1,0:T(1,128)} %shift_hbm.1, ...), custom_call_target="tpu_custom_call" | custom-call | tf_op jit(solution)/shard_map/pallas_call | solution.py:510
  108.2 1.0 copy.11

commit v7 on v5

--- a/solution.py
+++ b/solution.py
@@ -449,6 +449,28 @@
     def _():
         for tick in range(TICKS - 1):
             collect(tick)
+
+
+def write_kernel(source, target, sem):
+    copies = [
+        pltpu.make_async_copy(source.at[tick], target.at[tick], sem.at[tick])
+        for tick in range(TICKS)
+    ]
+    for copy in copies:
+        copy.start()
+    for copy in copies:
+        copy.wait()
+
+
+def write_out(result):
+    return pl.pallas_call(
+        write_kernel,
+        out_shape=jax.ShapeDtypeStruct(result.shape, result.dtype),
+        in_specs=[pl.BlockSpec(memory_space=pltpu.VMEM)],
+        out_specs=pl.BlockSpec(memory_space=pl.ANY),
+        scratch_shapes=[pltpu.SemaphoreType.DMA((TICKS,))],
+        compiler_params=pltpu.CompilerParams(vmem_limit_bytes=VMEM_BYTES // 8),
+    )(result)
 
 
 def relay_call(n, sections, pieces, hop_slots, args):
@@ -508,7 +530,7 @@
         patches.reshape(micro, pieces, rows, width),
         plan,
     )
-    return out.reshape(1, TICKS, tokens, width)
+    return write_out(out).reshape(1, TICKS, tokens, width)
 
 
 def passed_along(value, axis, steps):

time: 109 us -> 109 us (level)
  no operation moved by 1% of the time
where the time goes in v7:
time: 109 us
  Pallas kernels  109 us (100%)
    pallas_call x1, Pallas kernels, relay_call(): pl.pallas_call(functools.partial(relay_kernel, n, sections, hop_slots), o...  108 us

profile of v7, /device:TPU:17, one launch (start us, length us, event | category | flops | bytes accessed | tf_op | source)
XLA Modules:
  0.0 109.2 jit_solution(11787780278370991740)
XLA Ops:
  0.0 108.2 %shard_map.91.source = bf16[4,4,32,1024]{3,2,1,0:T(8,128)(2,1)S(1)} custom-call(bf16[4,32,1024]{2,1,0:T(8,128)(2,1)} %bitcast.8, bf16[576,1024]{1,0:T(8,128)(2,1)} %bitcast.6, bf16[1,576]{1,0:T(2,128)(2,1)} %ib_hbm.1, bf16[576,1024]{1,0:T(8,128)(2,1)} %bitcast.7, f32[1,1024]{1,0:T(1,128)} %ob_hbm.1, f32[1,1024]{1,0:T(1,128)} %gain_hbm.1, ...), custom_call_target="tpu_custom_call" | custom-call | tf_op jit(solution)/shard_map/pallas_call | solution.py:487
  108.2 1.0 shard_map.92
